TPU v7x, 32 devices: a whole 2x2x4 slice. The times are simulated.
32 devices in a mesh: blk: 16 (over z, y, core), tp: 2 (over x).
Axes of the slice: x: 2, y: 2, z: 4, core: 2. Of those that a mesh axis runs over, the one named last changes fastest.
Arguments:
- dec_states: bfloat16 [4096, 5120], P('blk', 'tp'), may hold values from -200 to 200
- norm_gain: float32 [5120], replicated, may hold values from 0.1 to 1.9
- query_weight: bfloat16 [5120, 768], P(None, 'tp'), may hold values from -0.078125 to 0.078125
- out_weight: bfloat16 [768, 5120], P('tp'), may hold values from -0.21875 to 0.21875
- enc_keys: bfloat16 [6144, 768], P('blk', 'tp'), may hold values from -1000 to 1000
- enc_values: bfloat16 [6144, 768], P('blk', 'tp'), may hold values from -6 to 6
Outputs:
- attn_out: bfloat16 [4096, 5120], P('blk', 'tp')
All inputs are finite; a program needn't handle non-finite values.
Results may differ from a plain program's by a relative error of at most 0.034.
Values may be sent and summed in bfloat16 or wider, within the bound.
A program may use at most 128 MiB of HBM per device.

v0:
```python
import math
import jax
import jax.numpy as jnp
from jax import lax
from jax.sharding import PartitionSpec as P

HEAD_DIM = 128
NORM_EPS = 1e-06


def block_rows(total_rows, shard_rows, limit):
    shards = total_rows // shard_rows
    chosen = 1
    for count_try in range(1, shards + 1):
        if shards % count_try == 0 and count_try * shard_rows <= limit:
            chosen = count_try
    return chosen * shard_rows


def per_device(dec_states, norm_gain, query_weight, out_weight, enc_keys, enc_values):
    heads = query_weight.shape[1] // HEAD_DIM
    q_rows = dec_states.shape[0]
    score_scale = 1.0 / math.sqrt(HEAD_DIM)
    states = lax.all_gather(dec_states, "tp", axis=1, tiled=True).astype(jnp.float32)
    mean_sq = jnp.mean(states * states, axis=1, keepdims=True)
    normed = (states * lax.rsqrt(mean_sq + NORM_EPS) * norm_gain).astype(jnp.bfloat16)
    queries = jnp.dot(normed, query_weight, preferred_element_type=jnp.float32).astype(jnp.bfloat16)
    query_heads = queries.reshape(q_rows, heads, HEAD_DIM)
    shard_rows = enc_keys.shape[0]
    start_state = (
        jnp.full((heads, q_rows), -1e30, jnp.float32),
        jnp.zeros((heads, q_rows), jnp.float32),
        jnp.zeros((heads, q_rows, HEAD_DIM), jnp.float32),
    )
    key_rows = lax.all_gather(enc_keys, "blk", axis=0, tiled=True)
    value_rows = lax.all_gather(enc_values, "blk", axis=0, tiled=True)
    count = key_rows.shape[0]
    width_rows = block_rows(count, shard_rows, 1536)
    key_blocks = key_rows.reshape(count // width_rows, width_rows, heads, HEAD_DIM)
    value_blocks = value_rows.reshape(count // width_rows, width_rows, heads, HEAD_DIM)

    def step_block(state, blocks):
        row_max, row_sum, summed = state
        key_block, value_block = blocks
        scores = (
            jnp.einsum("qhd,khd->hqk", query_heads, key_block, preferred_element_type=jnp.float32)
            * score_scale
        )
        new_max = jnp.maximum(row_max, jnp.max(scores, axis=2))
        factor = jnp.exp(row_max - new_max)
        exp_scores = jnp.exp(scores - new_max[:, :, None])
        new_sum = row_sum * factor + jnp.sum(exp_scores, axis=2)
        mixed = jnp.einsum(
            "hqk,khd->hqd",
            exp_scores.astype(jnp.bfloat16),
            value_block,
            preferred_element_type=jnp.float32,
        )
        return ((new_max, new_sum, summed * factor[:, :, None] + mixed), None)

    result, unused = lax.scan(step_block, start_state, (key_blocks, value_blocks))
    row_max, row_sum, summed = result
    attended = (
        (summed / row_sum[:, :, None])
        .transpose(1, 0, 2)
        .reshape(q_rows, heads * HEAD_DIM)
        .astype(jnp.bfloat16)
    )
    partial_out = jnp.dot(attended, out_weight, preferred_element_type=jnp.float32)
    return lax.psum_scatter(partial_out.astype(jnp.bfloat16), "tp", scatter_dimension=1, tiled=True)


def solution(mesh):
    in_specs = (P("blk", "tp"), P(), P(None, "tp"), P("tp", None), P("blk", "tp"), P("blk", "tp"))
    out_specs = P("blk", "tp")
    return jax.shard_map(
        per_device, mesh=mesh, in_specs=in_specs, out_specs=out_specs, check_vma=False
    )
```

profile of v0, /device:TPU:0, one launch (start us, length us, event | category | flops | bytes accessed | tf_op | source)
XLA Modules:
  0.0 269.0 jit_solution(2074089705996655652)
XLA Ops:
  6.5 0.7 all-gather.6.cloned.1.call-update
  7.3 0.7 all-gather.4.cloned.1.call-update
  8.1 0.7 all-gather.8.cloned.1.call-update
  8.8 41.8 %all-gather.6.cloned.1.call-done = bf16[256,5120]{1,0:T(8,128)(2,1)} async-done(((bf16[256,2560]{1,0:T(8,128)(2,1)}), bf16[256,5120]{1,0:T(8,128)(2,1)}) %all-gather.6.cloned.1.call-update) | async-done | bytes 2621456 | tf_op jit(solution)/shard_map/all_gather | solution.py:24
  50.6 2.3 fusion.19
  53.0 4.5 %fusion.26 = bf16[256,384]{1,0:T(8,128)(2,1)S(1)} fusion(bf16[5120,384]{1,0:T(8,128)(2,1)} %param.10, bf16[256,5120]{1,0:T(8,128)(2,1)} %all-gather.6.cloned.1.call-done, f32[5120]{0:T(1024)} %param.9, f32[256]{0:T(256)S(1)} %add_rsqrt_fusion), kind=kOutput, calls=%fused_computation.31 | convolution fusion | flops 1011974144 | bytes 6771712 | tf_op jit(solution)/shard_map/dot_general | solution.py:27
  57.8 48.3 %all-gather.4.cloned.1.call-done = bf16[6144,384]{1,0:T(8,128)(2,1)} async-done(((bf16[384,384]{1,0:T(8,128)(2,1)}), bf16[6144,384]{1,0:T(8,128)(2,1)}) %all-gather.4.cloned.1.call-update) | async-done | bytes 4718608 | tf_op jit(solution)/shard_map/all_gather | solution.py:35
  106.1 13.0 %reshape.26 = bf16[4,1536,3,128]{3,2,1,0:T(4,128)(2,1)} reshape(bf16[6144,384]{1,0:T(8,128)(2,1)} %all-gather.4.cloned.1.call-done) | data formatting | bytes 9437184 | tf_op jit(solution)/shard_map/reshape | solution.py:39
  119.0 6.0 %copy.13 = bf16[4,1536,3,128]{3,1,2,0:T(8,128)(2,1)} copy(bf16[4,1536,3,128]{3,2,1,0:T(4,128)(2,1)} %reshape.26) | data formatting | bytes 9437184
  125.0 35.0 %all-gather.8.cloned.1.call-done = bf16[6144,384]{1,0:T(8,128)(2,1)} async-done(((bf16[384,384]{1,0:T(8,128)(2,1)}), bf16[6144,384]{1,0:T(8,128)(2,1)}) %all-gather.8.cloned.1.call-update) | async-done | bytes 4718608 | tf_op jit(solution)/shard_map/all_gather | solution.py:36
  160.1 12.9 %reshape.27 = bf16[4,1536,3,128]{3,2,1,0:T(4,128)(2,1)} reshape(bf16[6144,384]{1,0:T(8,128)(2,1)} %all-gather.8.cloned.1.call-done) | data formatting | bytes 9437184 | tf_op jit(solution)/shard_map/reshape | solution.py:40
  173.0 6.0 %copy.15 = bf16[4,1536,3,128]{3,1,2,0:T(8,128)(2,1)} copy(bf16[4,1536,3,128]{3,2,1,0:T(4,128)(2,1)} %reshape.27) | data formatting | bytes 9437184
  179.0 41.7 %while.15 = (s32[]{:T(128)}, f32[3,256]{1,0:T(4,128)S(1)}, f32[3,256]{1,0:T(4,128)S(1)}, f32[3,256,128]{2,1,0:T(8,128)S(1)}, bf16[4,1536,3,128]{3,1,2,0:T(8,128)...) while((s32[]{:T(128)}, f32[3,256]{1,0:T(4,128)S(1)}, ...), condition=%wide.region_4.5_spmd.clone, body=%wide.region_1.4_spmd.clone.sunk | while | flops 613715712 | bytes 36422788 | solution.py:61
  179.0 4.2 %bitcast_reduce_fusion.2 = (f32[3,256]{1,0:T(4,128)S(1)}, f32[3,1536,256]{2,1,0:T(8,128)}) fusion(bf16[256,3,128]{2,0,1:T(8,128)(2,1)S(1)} %get-tuple-element.175, bf16[4,1536,3,128]{3,1,2,0:T(8,128)(2,1)} %get-tuple-element.174, s32[]{:T(128)} %get-tuple-element.161), kind=kOutput, calls=%fused_computation.1.clone.1 | convolution fusion | flops 304348416 | bytes 6098432 | tf_op jit(solution)/shard_map/while/body/eval_jaxpr/qhd,khd->hqk/dot_general | solution.py:46
  183.2 3.3 %fusion.42 = f32[3,256]{1,0:T(4,128)S(1)} fusion(f32[3,1536,256]{2,1,0:T(8,128)} %get-tuple-element.149, f32[3,256]{1,0:T(4,128)S(1)} %select_maximum_fusion.2), kind=kLoop, calls=%fused_computation.4.clone.1 | loop fusion | flops 3538176 | bytes 4724736 | tf_op jit(solution)/shard_map/while/body/eval_jaxpr/reduce_sum | solution.py:52
  186.4 0.5 copy-done
  186.9 2.5 fusion.44
  189.4 4.2 %bitcast_reduce_fusion.2 = (f32[3,256]{1,0:T(4,128)S(1)}, f32[3,1536,256]{2,1,0:T(8,128)}) fusion(bf16[256,3,128]{2,0,1:T(8,128)(2,1)S(1)} %get-tuple-element.175, bf16[4,1536,3,128]{3,1,2,0:T(8,128)(2,1)} %get-tuple-element.174, s32[]{:T(128)} %get-tuple-element.161), kind=kOutput, calls=%fused_computation.1.clone.1 | convolution fusion | flops 304348416 | bytes 6098432 | tf_op jit(solution)/shard_map/while/body/eval_jaxpr/qhd,khd->hqk/dot_general | solution.py:46
  193.6 3.3 %fusion.42 = f32[3,256]{1,0:T(4,128)S(1)} fusion(f32[3,1536,256]{2,1,0:T(8,128)} %get-tuple-element.149, f32[3,256]{1,0:T(4,128)S(1)} %select_maximum_fusion.2), kind=kLoop, calls=%fused_computation.4.clone.1 | loop fusion | flops 3538176 | bytes 4724736 | tf_op jit(solution)/shard_map/while/body/eval_jaxpr/reduce_sum | solution.py:52
  196.9 0.5 copy-done
  197.3 2.5 fusion.44
  199.9 4.2 %bitcast_reduce_fusion.2 = (f32[3,256]{1,0:T(4,128)S(1)}, f32[3,1536,256]{2,1,0:T(8,128)}) fusion(bf16[256,3,128]{2,0,1:T(8,128)(2,1)S(1)} %get-tuple-element.175, bf16[4,1536,3,128]{3,1,2,0:T(8,128)(2,1)} %get-tuple-element.174, s32[]{:T(128)} %get-tuple-element.161), kind=kOutput, calls=%fused_computation.1.clone.1 | convolution fusion | flops 304348416 | bytes 6098432 | tf_op jit(solution)/shard_map/while/body/eval_jaxpr/qhd,khd->hqk/dot_general | solution.py:46
  204.0 3.3 %fusion.42 = f32[3,256]{1,0:T(4,128)S(1)} fusion(f32[3,1536,256]{2,1,0:T(8,128)} %get-tuple-element.149, f32[3,256]{1,0:T(4,128)S(1)} %select_maximum_fusion.2), kind=kLoop, calls=%fused_computation.4.clone.1 | loop fusion | flops 3538176 | bytes 4724736 | tf_op jit(solution)/shard_map/while/body/eval_jaxpr/reduce_sum | solution.py:52
  207.3 0.5 copy-done
  207.8 2.5 fusion.44
  210.3 4.2 %bitcast_reduce_fusion.2 = (f32[3,256]{1,0:T(4,128)S(1)}, f32[3,1536,256]{2,1,0:T(8,128)}) fusion(bf16[256,3,128]{2,0,1:T(8,128)(2,1)S(1)} %get-tuple-element.175, bf16[4,1536,3,128]{3,1,2,0:T(8,128)(2,1)} %get-tuple-element.174, s32[]{:T(128)} %get-tuple-element.161), kind=kOutput, calls=%fused_computation.1.clone.1 | convolution fusion | flops 304348416 | bytes 6098432 | tf_op jit(solution)/shard_map/while/body/eval_jaxpr/qhd,khd->hqk/dot_general | solution.py:46
  214.5 3.3 %fusion.42 = f32[3,256]{1,0:T(4,128)S(1)} fusion(f32[3,1536,256]{2,1,0:T(8,128)} %get-tuple-element.149, f32[3,256]{1,0:T(4,128)S(1)} %select_maximum_fusion.2), kind=kLoop, calls=%fused_computation.4.clone.1 | loop fusion | flops 3538176 | bytes 4724736 | tf_op jit(solution)/shard_map/while/body/eval_jaxpr/reduce_sum | solution.py:52
  217.8 0.5 copy-done
  218.2 2.5 fusion.44
  220.7 0.2 copy.16
  220.9 5.2 %convolution_convert_fusion = bf16[256,5120]{1,0:T(8,128)(2,1)} fusion(bf16[256,384]{0,1:T(8,128)(2,1)S(1)} %bitcast.40, bf16[384,5120]{1,0:T(8,128)(2,1)} %param.11), kind=kOutput, calls=%fused_computation.24 | convolution fusion | flops 1007943680 | bytes 6750208 | tf_op jit(solution)/shard_map/dot_general | solution.py:69
  226.1 36.4 %reduce-scatter.2.cloned.1.call-done = bf16[256,2560]{1,0:T(8,128)(2,1)} async-done(((bf16[256,5120]{1,0:T(8,128)(2,1)}), bf16[256,2560]{1,0:T(8,128)(2,1)}) %reduce-scatter.2.cloned.1.call-update) | async-done | bytes 1310736 | tf_op jit(solution)/shard_map/reduce_scatter | solution.py:70
  (28 shorter events, 0.6 us)
Async XLA Ops:
  6.5 44.1 %all-gather.6.cloned.1.call-start = ((), (), s32[]{:S(2)}) async-start(), calls=%async_computation.2 | async-start | bytes 3932160 | tf_op jit(solution)/shard_map/all_gather | solution.py:24
  7.3 98.8 %all-gather.4.cloned.1.call-start = ((), (), s32[]{:S(2)}) async-start(), calls=%async_computation.1 | async-start | bytes 5013504 | tf_op jit(solution)/shard_map/all_gather | solution.py:35
  8.0 152.0 %all-gather.8.cloned.1.call-start = ((), (), s32[]{:S(2)}) async-start(), calls=%async_computation.3 | async-start | bytes 5013504 | tf_op jit(solution)/shard_map/all_gather | solution.py:36
  8.7 253.8 %reduce-scatter.2.cloned.1.call-start = ((), (), s32[]{:S(2)}) async-start(), calls=%async_computation.4 | async-start | bytes 3932160 | tf_op jit(solution)/shard_map/reduce_scatter | solution.py:70
  183.1 3.8 %copy-start = (f32[3,1536,256]{2,1,0:T(8,128)S(1)}, f32[3,1536,256]{2,1,0:T(8,128)}, u32[]{:S(2)}) copy-start(f32[3,1536,256]{2,1,0:T(8,128)} %get-tuple-element.149) | copy-start | bytes 14155780 | tf_op jit(solution)/shard_map/while
  193.6 3.8 %copy-start = (f32[3,1536,256]{2,1,0:T(8,128)S(1)}, f32[3,1536,256]{2,1,0:T(8,128)}, u32[]{:S(2)}) copy-start(f32[3,1536,256]{2,1,0:T(8,128)} %get-tuple-element.149) | copy-start | bytes 14155780 | tf_op jit(solution)/shard_map/while
  204.0 3.8 %copy-start = (f32[3,1536,256]{2,1,0:T(8,128)S(1)}, f32[3,1536,256]{2,1,0:T(8,128)}, u32[]{:S(2)}) copy-start(f32[3,1536,256]{2,1,0:T(8,128)} %get-tuple-element.149) | copy-start | bytes 14155780 | tf_op jit(solution)/shard_map/while
  214.5 3.8 %copy-start = (f32[3,1536,256]{2,1,0:T(8,128)S(1)}, f32[3,1536,256]{2,1,0:T(8,128)}, u32[]{:S(2)}) copy-start(f32[3,1536,256]{2,1,0:T(8,128)} %get-tuple-element.149) | copy-start | bytes 14155780 | tf_op jit(solution)/shard_map/while
Sparse Core Ops, SparseCore 0:
  8.9 41.7 all-gather.5
  52.9 53.1 all-gather.3
  108.4 51.6 all-gather.7
  226.2 36.2 reduce-scatter.1
where the time goes:
time: 270 us; the launch traced here: 269 us
  waiting for transfers between devices  164 us (61%)
  local copies, waits for them, and re-layouts  40.2 us (15%)
  matrix products  36.3 us (13%)
  other arithmetic  15.6 us (6%)
  between operations  13.2 us (5%)
    all_gather x1, waiting for transfers between devices, per_device(): key_rows = lax.all_gather(enc_keys, 'blk', axis=0, tiled=True)  48.3 us
    all_gather x1, waiting for transfers between devices, per_device(): lax.all_gather(dec_states, 'tp', axis=1, tiled=True).astype(jnp.float32)  41.8 us
    reduce_scatter x1, waiting for transfers between devices, per_device(): lax.psum_scatter(partial_out.astype(jnp.bfloat16), 'tp', scatter_dimensio...  36.4 us
    all_gather x1, waiting for transfers between devices, per_device(): value_rows = lax.all_gather(enc_values, 'blk', axis=0, tiled=True)  35 us
    dot_general x4, matrix products, step_block(): jnp.einsum('qhd,khd->hqk', query_heads, key_block, preferred_element_type...  16.7 us
    reduce_sum x4, other arithmetic, step_block(): new_sum = row_sum * factor + jnp.sum(exp_scores, axis=2)  13.1 us
    reshape x1, local copies, waits for them, and re-layouts, per_device(): key_rows.reshape(count // width_rows, width_rows, heads, HEAD_DIM)  13 us
    reshape x1, local copies, waits for them, and re-layouts, per_device(): value_rows.reshape(count // width_rows, width_rows, heads, HEAD_DIM)  12.9 us
  transfers between devices with their start and end apart: 4, of which 4 were waited for; matrix products, arithmetic and copies ran while one was open for 10% of the time, Pallas kernels for 0%

commit v1 on v0

--- a/solution.py
+++ b/solution.py
@@ -6,6 +6,7 @@
 
 HEAD_DIM = 128
 NORM_EPS = 1e-06
+unite_weights_in = lambda obj: jnp.concatenate(lax.all_gather(obj, "tp"), axis=1)
 
 
 def block_rows(total_rows, shard_rows, limit):
@@ -21,7 +22,7 @@
     heads = query_weight.shape[1] // HEAD_DIM
     q_rows = dec_states.shape[0]
     score_scale = 1.0 / math.sqrt(HEAD_DIM)
-    states = lax.all_gather(dec_states, "tp", axis=1, tiled=True).astype(jnp.float32)
+    states = unite_weights_in(dec_states).astype(jnp.float32)
     mean_sq = jnp.mean(states * states, axis=1, keepdims=True)
     normed = (states * lax.rsqrt(mean_sq + NORM_EPS) * norm_gain).astype(jnp.bfloat16)
     queries = jnp.dot(normed, query_weight, preferred_element_type=jnp.float32).astype(jnp.bfloat16)

time: 270 us -> 270 us (level)
  waiting for transfers between devices: 164 us -> 153 us
  other arithmetic: 15.6 us -> 22.8 us
  local copies, waits for them, and re-layouts: 40.2 us -> 46.2 us
  matrix products: 36.3 us -> 33.4 us
    all_gather x1, waiting for transfers between devices: 48.3 us -> 37.9 us  [per_device(): key_rows = lax.all_gather(enc_keys, 'blk', axis=0, tiled=True)]
    convert_element_type x0 -> x2, other arithmetic: none -> 8.96 us  [the longest x1 4.75 us: per_device(): states = unite_weights_in(dec_states).astype(jnp.float32)]
    convert_element_type x0 -> x1, local copies, waits for them, and re-layouts: none -> 6.05 us  [per_device(): states = unite_weights_in(dec_states).astype(jnp.float32)]
    dot_general x1, matrix products: 4.52 us -> 1.56 us  [per_device(): jnp.dot(normed, query_weight, preferred_element_type=jnp.float32)]
    unnamed x3 -> x9, local copies, waits for them, and re-layouts: 12.2 us -> 12.1 us
  transfers between devices with their start and end apart: 4 -> 4, of which waited for: 4 -> 4; matrix products, arithmetic and copies ran while one was open for 10% -> 14% of each run, Pallas kernels for 0% -> 0%
where the time goes in v1:
time: 270 us; the launch traced here: 269 us
  waiting for transfers between devices  153 us (57%)
  local copies, waits for them, and re-layouts  46.2 us (17%)
  matrix products  33.4 us (12%)
  other arithmetic  22.8 us (8%)
  between operations  13.2 us (5%)
    all_gather x1, waiting for transfers between devices, lax.all_gather(obj, 'tp')  41.8 us
    all_gather x1, waiting for transfers between devices, per_device(): key_rows = lax.all_gather(enc_keys, 'blk', axis=0, tiled=True)  37.9 us
    reduce_scatter x1, waiting for transfers between devices, per_device(): lax.psum_scatter(partial_out.astype(jnp.bfloat16), 'tp', scatter_dimensio...  36.4 us
    all_gather x1, waiting for transfers between devices, per_device(): value_rows = lax.all_gather(enc_values, 'blk', axis=0, tiled=True)  35.1 us
    dot_general x4, matrix products, step_block(): jnp.einsum('qhd,khd->hqk', query_heads, key_block, preferred_element_type...  16.8 us
    reduce_sum x4, other arithmetic, step_block(): new_sum = row_sum * factor + jnp.sum(exp_scores, axis=2)  13.1 us
    reshape x1, local copies, waits for them, and re-layouts, per_device(): key_rows.reshape(count // width_rows, width_rows, heads, HEAD_DIM)  12.9 us
    reshape x1, local copies, waits for them, and re-layouts, per_device(): value_rows.reshape(count // width_rows, width_rows, heads, HEAD_DIM)  12.9 us
  transfers between devices with their start and end apart: 4, of which 4 were waited for; matrix products, arithmetic and copies ran while one was open for 14% of the time, Pallas kernels for 0%

profile of v1, /device:TPU:0, one launch (start us, length us, event | category | flops | bytes accessed | tf_op | source)
XLA Modules:
  0.0 269.2 jit_solution(13535137969171957085)
XLA Ops:
  6.5 0.7 all-gather.9.cloned.1.call-update
  7.3 0.7 all-gather.5.cloned.1.call-update
  8.1 0.7 all-gather.7.cloned.1.call-update
  8.8 41.8 %all-gather.9.cloned.1.call-done = bf16[512,2560]{1,0:T(8,128)(2,1)} async-done(((bf16[256,2560]{1,0:T(8,128)(2,1)}), bf16[512,2560]{1,0:T(8,128)(2,1)}) %all-gather.9.cloned.1.call-update) | async-done | bytes 2621456 | tf_op jit(solution)/shard_map/all_gather | solution.py:9
  50.6 4.8 %convert_bitcast_fusion = f32[256,2,2560]{2,0,1:T(8,128)} fusion(bf16[512,2560]{1,0:T(8,128)(2,1)} %all-gather.9.cloned.1.call-done), kind=kLoop, calls=%fused_computation.23 | loop fusion | flops 1310720 | bytes 7864320 | tf_op jit(solution)/shard_map/convert_element_type | solution.py:25
  55.4 6.1 %copy.19 = f32[256,2,2560]{0,2,1:T(8,128)} copy(f32[256,2,2560]{2,0,1:T(8,128)} %convert_bitcast_fusion) | data formatting | bytes 10485760 | tf_op jit(solution)/shard_map/convert_element_type | solution.py:25
  61.4 0.6 fusion.19
  62.1 4.2 %fusion.21 = bf16[256,5120]{0,1:T(8,128)(2,1)S(1)} fusion(f32[256,2,2560]{0,2,1:T(8,128)} %copy.19, f32[5120]{0:T(1024)S(1)} %copy-done.2, f32[256]{0:T(256)S(1)} %add_rsqrt_fusion), kind=kLoop, calls=%fused_computation.28 | loop fusion | flops 3932160 | bytes 7885824 | tf_op jit(solution)/shard_map/convert_element_type | solution.py:27
  66.3 1.6 convolution_convert_fusion.1
  68.2 37.9 %all-gather.5.cloned.1.call-done = bf16[6144,384]{1,0:T(8,128)(2,1)} async-done(((bf16[384,384]{1,0:T(8,128)(2,1)}), bf16[6144,384]{1,0:T(8,128)(2,1)}) %all-gather.5.cloned.1.call-update) | async-done | bytes 4718608 | tf_op jit(solution)/shard_map/all_gather | solution.py:36
  106.1 12.9 %reshape.34 = bf16[4,1536,3,128]{3,2,1,0:T(4,128)(2,1)} reshape(bf16[6144,384]{1,0:T(8,128)(2,1)} %all-gather.5.cloned.1.call-done) | data formatting | bytes 9437184 | tf_op jit(solution)/shard_map/reshape | solution.py:40
  119.0 5.9 %copy.22 = bf16[4,1536,3,128]{3,1,2,0:T(8,128)(2,1)} copy(bf16[4,1536,3,128]{3,2,1,0:T(4,128)(2,1)} %reshape.34) | data formatting | bytes 9437184
  124.9 35.1 %all-gather.7.cloned.1.call-done = bf16[6144,384]{1,0:T(8,128)(2,1)} async-done(((bf16[384,384]{1,0:T(8,128)(2,1)}), bf16[6144,384]{1,0:T(8,128)(2,1)}) %all-gather.7.cloned.1.call-update) | async-done | bytes 4718608 | tf_op jit(solution)/shard_map/all_gather | solution.py:37
  160.1 12.9 %reshape.35 = bf16[4,1536,3,128]{3,2,1,0:T(4,128)(2,1)} reshape(bf16[6144,384]{1,0:T(8,128)(2,1)} %all-gather.7.cloned.1.call-done) | data formatting | bytes 9437184 | tf_op jit(solution)/shard_map/reshape | solution.py:41
  173.0 6.0 %copy.24 = bf16[4,1536,3,128]{3,1,2,0:T(8,128)(2,1)} copy(bf16[4,1536,3,128]{3,2,1,0:T(4,128)(2,1)} %reshape.35) | data formatting | bytes 9437184
  179.0 41.8 %while.15 = (s32[]{:T(128)}, f32[3,256]{1,0:T(4,128)S(1)}, f32[3,256]{1,0:T(4,128)S(1)}, f32[3,256,128]{2,1,0:T(8,128)S(1)}, bf16[4,1536,3,128]{3,1,2,0:T(8,128)...) while((s32[]{:T(128)}, f32[3,256]{1,0:T(4,128)S(1)}, ...), condition=%wide.region_4.5_spmd.clone, body=%wide.region_1.4_spmd.clone.sunk | while | flops 613715712 | bytes 36422788 | solution.py:62
  179.0 4.2 %bitcast_reduce_fusion.2 = (f32[3,256]{1,0:T(4,128)S(1)}, f32[3,1536,256]{2,1,0:T(8,128)}) fusion(bf16[256,3,128]{2,0,1:T(8,128)(2,1)S(1)} %get-tuple-element.182, bf16[4,1536,3,128]{3,1,2,0:T(8,128)(2,1)} %get-tuple-element.181, s32[]{:T(128)} %get-tuple-element.168), kind=kOutput, calls=%fused_computation.1.clone.1 | convolution fusion | flops 304348416 | bytes 6098432 | tf_op jit(solution)/shard_map/while/body/eval_jaxpr/qhd,khd->hqk/dot_general | solution.py:47
  183.2 3.3 %fusion.36 = f32[3,256]{1,0:T(4,128)S(1)} fusion(f32[3,1536,256]{2,1,0:T(8,128)} %get-tuple-element.156, f32[3,256]{1,0:T(4,128)S(1)} %select_maximum_fusion.2), kind=kLoop, calls=%fused_computation.4.clone.1 | loop fusion | flops 3538176 | bytes 4724736 | tf_op jit(solution)/shard_map/while/body/eval_jaxpr/reduce_sum | solution.py:53
  186.5 0.5 copy-done
  186.9 2.5 fusion.38
  189.5 4.2 %bitcast_reduce_fusion.2 = (f32[3,256]{1,0:T(4,128)S(1)}, f32[3,1536,256]{2,1,0:T(8,128)}) fusion(bf16[256,3,128]{2,0,1:T(8,128)(2,1)S(1)} %get-tuple-element.182, bf16[4,1536,3,128]{3,1,2,0:T(8,128)(2,1)} %get-tuple-element.181, s32[]{:T(128)} %get-tuple-element.168), kind=kOutput, calls=%fused_computation.1.clone.1 | convolution fusion | flops 304348416 | bytes 6098432 | tf_op jit(solution)/shard_map/while/body/eval_jaxpr/qhd,khd->hqk/dot_general | solution.py:47
  193.7 3.3 %fusion.36 = f32[3,256]{1,0:T(4,128)S(1)} fusion(f32[3,1536,256]{2,1,0:T(8,128)} %get-tuple-element.156, f32[3,256]{1,0:T(4,128)S(1)} %select_maximum_fusion.2), kind=kLoop, calls=%fused_computation.4.clone.1 | loop fusion | flops 3538176 | bytes 4724736 | tf_op jit(solution)/shard_map/while/body/eval_jaxpr/reduce_sum | solution.py:53
  197.4 2.5 fusion.38
  199.9 4.2 %bitcast_reduce_fusion.2 = (f32[3,256]{1,0:T(4,128)S(1)}, f32[3,1536,256]{2,1,0:T(8,128)}) fusion(bf16[256,3,128]{2,0,1:T(8,128)(2,1)S(1)} %get-tuple-element.182, bf16[4,1536,3,128]{3,1,2,0:T(8,128)(2,1)} %get-tuple-element.181, s32[]{:T(128)} %get-tuple-element.168), kind=kOutput, calls=%fused_computation.1.clone.1 | convolution fusion | flops 304348416 | bytes 6098432 | tf_op jit(solution)/shard_map/while/body/eval_jaxpr/qhd,khd->hqk/dot_general | solution.py:47
  204.1 3.3 %fusion.36 = f32[3,256]{1,0:T(4,128)S(1)} fusion(f32[3,1536,256]{2,1,0:T(8,128)} %get-tuple-element.156, f32[3,256]{1,0:T(4,128)S(1)} %select_maximum_fusion.2), kind=kLoop, calls=%fused_computation.4.clone.1 | loop fusion | flops 3538176 | bytes 4724736 | tf_op jit(solution)/shard_map/while/body/eval_jaxpr/reduce_sum | solution.py:53
  207.9 2.5 fusion.38
  210.4 4.2 %bitcast_reduce_fusion.2 = (f32[3,256]{1,0:T(4,128)S(1)}, f32[3,1536,256]{2,1,0:T(8,128)}) fusion(bf16[256,3,128]{2,0,1:T(8,128)(2,1)S(1)} %get-tuple-element.182, bf16[4,1536,3,128]{3,1,2,0:T(8,128)(2,1)} %get-tuple-element.181, s32[]{:T(128)} %get-tuple-element.168), kind=kOutput, calls=%fused_computation.1.clone.1 | convolution fusion | flops 304348416 | bytes 6098432 | tf_op jit(solution)/shard_map/while/body/eval_jaxpr/qhd,khd->hqk/dot_general | solution.py:47
  214.6 3.3 %fusion.36 = f32[3,256]{1,0:T(4,128)S(1)} fusion(f32[3,1536,256]{2,1,0:T(8,128)} %get-tuple-element.156, f32[3,256]{1,0:T(4,128)S(1)} %select_maximum_fusion.2), kind=kLoop, calls=%fused_computation.4.clone.1 | loop fusion | flops 3538176 | bytes 4724736 | tf_op jit(solution)/shard_map/while/body/eval_jaxpr/reduce_sum | solution.py:53
  217.9 0.5 copy-done
  218.3 2.5 fusion.38
  221.0 5.2 %convolution_convert_fusion = bf16[256,5120]{1,0:T(8,128)(2,1)} fusion(bf16[256,384]{0,1:T(8,128)(2,1)S(1)} %bitcast.53, bf16[384,5120]{1,0:T(8,128)(2,1)} %param.11), kind=kOutput, calls=%fused_computation.24 | convolution fusion | flops 1007943680 | bytes 6750208 | tf_op jit(solution)/shard_map/dot_general | solution.py:70
  226.3 36.4 %reduce-scatter.2.cloned.1.call-done = bf16[256,2560]{1,0:T(8,128)(2,1)} async-done(((bf16[256,5120]{1,0:T(8,128)(2,1)}), bf16[256,2560]{1,0:T(8,128)(2,1)}) %reduce-scatter.2.cloned.1.call-update) | async-done | bytes 1310736 | tf_op jit(solution)/shard_map/reduce_scatter | solution.py:71
  (37 shorter events, 1.7 us)
Async XLA Ops:
  6.5 44.1 %all-gather.9.cloned.1.call-start = ((), (), s32[]{:S(2)}) async-start(), calls=%async_computation.4 | async-start | bytes 3932160 | tf_op jit(solution)/shard_map/all_gather | solution.py:9
  7.3 98.8 %all-gather.5.cloned.1.call-start = ((), (), s32[]{:S(2)}) async-start(), calls=%async_computation.1 | async-start | bytes 5013504 | tf_op jit(solution)/shard_map/all_gather | solution.py:36
  8.0 152.0 %all-gather.7.cloned.1.call-start = ((), (), s32[]{:S(2)}) async-start(), calls=%async_computation.2 | async-start | bytes 5013504 | tf_op jit(solution)/shard_map/all_gather | solution.py:37
  8.7 253.9 %reduce-scatter.2.cloned.1.call-start = ((), (), s32[]{:S(2)}) async-start(), calls=%async_computation.3 | async-start | bytes 3932160 | tf_op jit(solution)/shard_map/reduce_scatter | solution.py:71
  55.4 6.1 %copy-start.1 = (bf16[512,2560]{1,0:T(8,128)(2,1)S(1)}, bf16[512,2560]{1,0:T(8,128)(2,1)}, u32[]{:S(2)}) copy-start(bf16[512,2560]{1,0:T(8,128)(2,1)} %all-gather.9.cloned.1.call-done) | copy-start | bytes 7864324
  55.4 6.7 %copy-start.2 = (f32[5120]{0:T(1024)S(1)}, f32[5120]{0:T(1024)}, u32[]{:S(2)}) copy-start(f32[5120]{0:T(1024)} %param.9) | copy-start | bytes 61444
  61.4 4.8 %copy-start.3 = (bf16[5120,384]{1,0:T(8,128)(2,1)S(1)}, bf16[5120,384]{1,0:T(8,128)(2,1)}, u32[]{:S(2)}) copy-start(bf16[5120,384]{1,0:T(8,128)(2,1)} %param.10) | copy-start | bytes 11796484
  183.2 3.8 %copy-start = (f32[3,1536,256]{2,1,0:T(8,128)S(1)}, f32[3,1536,256]{2,1,0:T(8,128)}, u32[]{:S(2)}) copy-start(f32[3,1536,256]{2,1,0:T(8,128)} %get-tuple-element.156) | copy-start | bytes 14155780 | tf_op jit(solution)/shard_map/while
  193.6 3.8 %copy-start = (f32[3,1536,256]{2,1,0:T(8,128)S(1)}, f32[3,1536,256]{2,1,0:T(8,128)}, u32[]{:S(2)}) copy-start(f32[3,1536,256]{2,1,0:T(8,128)} %get-tuple-element.156) | copy-start | bytes 14155780 | tf_op jit(solution)/shard_map/while
  204.1 3.8 %copy-start = (f32[3,1536,256]{2,1,0:T(8,128)S(1)}, f32[3,1536,256]{2,1,0:T(8,128)}, u32[]{:S(2)}) copy-start(f32[3,1536,256]{2,1,0:T(8,128)} %get-tuple-element.156) | copy-start | bytes 14155780 | tf_op jit(solution)/shard_map/while
  214.6 3.8 %copy-start = (f32[3,1536,256]{2,1,0:T(8,128)S(1)}, f32[3,1536,256]{2,1,0:T(8,128)}, u32[]{:S(2)}) copy-start(f32[3,1536,256]{2,1,0:T(8,128)} %get-tuple-element.156) | copy-start | bytes 14155780 | tf_op jit(solution)/shard_map/while
Sparse Core Ops, SparseCore 0:
  8.9 41.7 all-gather.8
  52.9 53.1 all-gather.4
  108.4 51.6 all-gather.6
  226.4 36.2 reduce-scatter.1
